TPU v7x, 32 devices: a whole 2x2x4 slice. The times are simulated.
32 devices in a mesh: grp: 8 (over y, x, core), sub: 4 (over z).
Axes of the slice: x: 2, y: 2, z: 4, core: 2. Of those that a mesh axis runs over, the one named last changes fastest.
Arguments:
- master: float32 [4096, 3584], P(('grp', 'sub')), may hold values from -120 to 120
- moment_one: float32 [4096, 3584], P(('grp', 'sub')), may hold values from -6 to 6
- moment_two: float32 [4096, 3584], P(('grp', 'sub')), may hold values from 0.01 to 4
- gradient: float32 [4096, 3584], P(('grp', 'sub')), may hold values from -120 to 120
- partner: int32 [32], replicated, may hold values from 0 to 31, each once
- tensor_of_row: int32 [4096], replicated, may hold values from 0 to 7, never falling along the last dimension, each value on 1 to 1024 neighbouring positions
Outputs:
- new_master: float32 [4096, 3584], P(('grp', 'sub'))
- new_moment_one: float32 [4096, 3584], P(('grp', 'sub'))
- new_moment_two: float32 [4096, 3584], P(('grp', 'sub'))
Inputs may be any that keep to these rules, and one draw needn't show every extreme that they name: partner[n] is the device of new rank n; every device holds exactly one rank. `tensor_of_row`: tensor numbers never fall along the rows; each of the 8 tensors has one or more rows.
All inputs are finite; a program needn't handle non-finite values.
Results may differ from a plain program's by a relative error of at most 0.00007.
Values sent between devices are 32-bit elements; how exact they have to be, the bound alone decides.
A program may use at most 128 MiB of HBM per device.

v0:
```python
import functools

import jax
import jax.numpy as jnp
from jax import lax
from jax.experimental import pallas as pl
from jax.experimental.pallas import tpu as pltpu
from jax.sharding import PartitionSpec as P

LAYERS = 8
LANES = 128
TILE = 8
PIECES = 4
MESH = pl.DeviceIdType.MESH

beta_one = 0.9
beta_two = 0.999
step_count = 10
adam_eps = 1e-06
trust_eps = 1e-06
learn_rate = 0.05
decay_rate = 0.01


def xor(a, b, bound):
    total, bit = 0, 1
    while bit < bound:
        total = total + ((a // bit + b // bit) % 2) * bit
        bit *= 2
    return total


def flips(here, bound):
    steps, bit = [], 1
    while bit < bound:
        steps.append(bit - 2 * bit * ((here // bit) % 2))
        bit *= 2
    return [
        here + sum(step for b, step in enumerate(steps) if (k >> b) % 2) for k in range(bound)
    ]


def sub_order(subs):
    width = subs.bit_length() - 1
    codes = [i ^ (i >> 1) for i in range(subs)]
    return [sum(((c >> b) & 1) << (width - 1 - b) for b in range(width)) for c in codes]


def prepare(groups, subs, partner, ids, master_hbm, one_hbm, two_hbm, staged, row_ids,
            master, one, two, load_sem):
    devices = groups * subs
    rows_dev, width = master.shape
    block = rows_dev // devices
    many = TILE // block
    me = lax.axis_index("grp") * subs + lax.axis_index("sub")
    loads = [
        pltpu.make_async_copy(src, dst, load_sem.at[i])
        for i, (src, dst) in enumerate([(master_hbm, master), (one_hbm, one), (two_hbm, two)])
    ]
    for load in loads:
        load.start()

    def rank_of(device):
        def seek(n, found):
            return found + jnp.where(partner[n] == device, n, 0)

        return lax.fori_loop(0, devices, seek, jnp.int32(0), unroll=8)

    my_rank = rank_of(me)
    sub_iota = lax.broadcasted_iota(jnp.int32, (TILE, LANES), 0)

    def name_rows(s):
        here = jnp.zeros((TILE, LANES), jnp.int32)
        for i in range(many):
            for b in range(block):
                tensor = ids[(s * many + i) * rows_dev + my_rank * block + b]
                here = jnp.where(sub_iota == i * block + b, tensor, here)
        row_ids[pl.ds(pl.multiple_of(s * TILE, TILE), TILE), :] = here

    for a, source in enumerate((master, one, two)):
        loads[a].wait()

        def stage(s, carry, a=a, source=source):
            rows = source[pl.ds(pl.multiple_of(s * TILE, TILE), TILE), :]
            for i in range(many):
                staged[partner[s * many + i], a] = rows[i * block : (i + 1) * block]
            if a == 0:
                name_rows(s)
            return carry

        lax.fori_loop(0, rows_dev // TILE, stage, 0)


def kernel(groups, subs, staged, row_ids, grad_hbm,
           weights, update, first_out, second_out, ratio_out,
           grad, landed, acc_w, acc_u, sums,
           load_sem, send_sem, recv_sem, sum_send, sum_recv):
    devices = groups * subs
    rows_dev, width = grad.shape
    block = rows_dev // devices
    many = TILE // block
    halves = subs // many
    columns = width // LANES
    my_grp, my_sub = lax.axis_index("grp"), lax.axis_index("sub")
    me = my_grp * subs + my_sub
    grps, sbs = flips(my_grp, groups), flips(my_sub, subs)
    order = sub_order(subs)
    peers = [g * subs + s for s in order for g in range(groups) if g or s]

    def at(k):
        return {"grp": grps[k // subs], "sub": sbs[k % subs]}

    load = pltpu.make_async_copy(grad_hbm, grad, load_sem)
    load.start()
    barrier = pltpu.get_barrier_semaphore()
    for k in reversed(peers):
        pl.semaphore_signal(barrier, inc=1, device_id=at(k), device_id_type=MESH)
    pl.semaphore_wait(barrier, devices - 1)

    def exchange(k):
        return pltpu.make_async_remote_copy(
            src_ref=staged.at[grps[k // subs] * subs + sbs[k % subs]],
            dst_ref=landed.at[k],
            send_sem=send_sem.at[k],
            recv_sem=recv_sem.at[k],
            device_id=at(k),
            device_id_type=MESH,
        )

    def exchange_sum(k):
        return pltpu.make_async_remote_copy(
            src_ref=sums.at[0],
            dst_ref=sums.at[k],
            send_sem=sum_send.at[k],
            recv_sem=sum_recv.at[k],
            device_id=at(k),
            device_id_type=MESH,
        )

    for k in peers:
        exchange(k).start()
    landed[0] = staged[me]
    load.wait()
    acc_w[...] = jnp.zeros_like(acc_w)
    acc_u[...] = jnp.zeros_like(acc_u)
    sub_iota = lax.broadcasted_iota(jnp.int32, (TILE, LANES), 0)
    lane_iota = lax.broadcasted_iota(jnp.int32, (TILE, LANES), 1)
    scale_one = 1.0 / (1.0 - beta_one**step_count)
    scale_two = 1.0 / (1.0 - beta_two**step_count)
    within = flips(me % many, many)

    def consume(j):
        base = pl.multiple_of(xor(me // many, j, devices // many) * TILE, TILE)
        slots = [j * many + within[i] for i in range(many)]
        here = row_ids[pl.ds(base, TILE), :]
        sum_w = jnp.zeros((TILE, LANES), jnp.float32)
        sum_u = jnp.zeros((TILE, LANES), jnp.float32)
        for c in range(columns):
            cut = slice(c * LANES, (c + 1) * LANES)

            def arrived(a):
                return jnp.concatenate([landed[slot, a, :, cut] for slot in slots], axis=0)

            g = grad[pl.ds(base, TILE), cut]
            w = arrived(0)
            first = beta_one * arrived(1) + (1.0 - beta_one) * g
            second = beta_two * arrived(2) + (1.0 - beta_two) * g * g
            u = (first * scale_one) / (jnp.sqrt(second * scale_two) + adam_eps) + decay_rate * w
            first_out[pl.ds(base, TILE), cut] = first
            second_out[pl.ds(base, TILE), cut] = second
            weights[pl.ds(base, TILE), cut] = w
            update[pl.ds(base, TILE), cut] = u
            sum_w += w * w
            sum_u += u * u
        for t in range(LAYERS):
            acc_w[t] += jnp.where(here == t, sum_w, 0.0)
            acc_u[t] += jnp.where(here == t, sum_u, 0.0)

    def receive(j, carry):
        for i in range(many):
            pltpu.make_async_remote_copy(
                src_ref=staged.at[0],
                dst_ref=landed.at[j * many + i],
                send_sem=send_sem.at[j * many + i],
                recv_sem=recv_sem.at[j * many + i],
                device_id=at(1),
                device_id_type=MESH,
            ).wait_recv()
        consume(j)
        return carry

    for h in sorted(range(halves), key=lambda h: max(order.index(h * many + i) for i in range(many))):
        if h == 0:
            for i in range(1, many):
                exchange(i).wait_recv()
            consume(0)
        lax.fori_loop(1 if h == 0 else 0, groups, lambda g, c, h=h: receive(g * halves + h, c), 0)

    col_w = jnp.sum(jnp.sum(acc_w[...], axis=1), axis=1, keepdims=True)
    col_u = jnp.sum(jnp.sum(acc_u[...], axis=1), axis=1, keepdims=True)
    spread = jnp.where(lane_iota == sub_iota, col_w, 0.0) + jnp.where(
        lane_iota == sub_iota + LAYERS, col_u, 0.0
    )
    sums[0] = jnp.sum(spread, axis=0, keepdims=True)
    for k in reversed(peers):
        exchange_sum(k).start()
    for k in peers:
        exchange(k).wait_send()
    for k in range(1, devices):
        exchange_sum(k).wait_recv()
    for k in range(1, devices):
        exchange_sum(k).wait_send()
    mine = flips(me, devices)
    total = jnp.zeros((1, LANES), jnp.float32)
    for o in range(devices):
        total = total + sums[mine[o]]
    wide = jnp.broadcast_to(total, (TILE, LANES))
    weight_sq = jnp.sum(jnp.where(lane_iota == sub_iota, wide, 0.0), axis=1, keepdims=True)
    update_sq = jnp.sum(jnp.where(lane_iota == sub_iota + LAYERS, wide, 0.0), axis=1, keepdims=True)
    ratio = learn_rate * (jnp.sqrt(weight_sq) / (jnp.sqrt(update_sq) + trust_eps))
    ratio_out[...] = jnp.broadcast_to(ratio, (TILE, LANES))


def finish(ratio_ref, row_ids, weights, update, first, second,
           fresh_hbm, first_hbm, second_hbm, fresh, fresh_sem, moment_sem):
    rows_dev, width = weights.shape
    columns = width // LANES
    moments = [
        pltpu.make_async_copy(first, first_hbm, moment_sem.at[0]),
        pltpu.make_async_copy(second, second_hbm, moment_sem.at[1]),
    ]
    for move in moments:
        move.start()
    ratio = ratio_ref[...]
    span = rows_dev // PIECES
    moves = []
    for p in range(PIECES):

        def step_rows(s, carry):
            base = pl.multiple_of(p * span + s * TILE, TILE)
            here = row_ids[pl.ds(base, TILE), :]
            step = jnp.zeros((TILE, LANES), jnp.float32)
            for t in range(LAYERS):
                step = jnp.where(here == t, jnp.broadcast_to(ratio[t : t + 1], (TILE, LANES)), step)
            for c in range(columns):
                cut = slice(c * LANES, (c + 1) * LANES)
                rows = pl.ds(base, TILE)
                fresh[rows, cut] = weights[rows, cut] - step * update[rows, cut]
            return carry

        lax.fori_loop(0, span // TILE, step_rows, 0)
        rows = pl.ds(p * span, span)
        moves.append(pltpu.make_async_copy(fresh.at[rows], fresh_hbm.at[rows], fresh_sem.at[p]))
        if p:
            moves[p - 1].start()
    moves[-1].start()
    for move in moves + moments:
        move.wait()


def local(groups, subs, master, moment_one, moment_two, gradient, partner, tensor_of_row):
    rows_dev, width = master.shape
    devices = groups * subs
    block = rows_dev // devices
    whole = jax.ShapeDtypeStruct((rows_dev, width), jnp.float32)
    vmem = pl.BlockSpec(memory_space=pltpu.VMEM)
    smem = pl.BlockSpec(memory_space=pltpu.SMEM)
    hbm = pl.BlockSpec(memory_space=pltpu.HBM)
    slots = (devices, 3, block, width)
    staged, row_ids = pl.pallas_call(
        functools.partial(prepare, groups, subs),
        out_shape=(
            pltpu.VMEM(slots, jnp.float32),
            pltpu.VMEM((rows_dev, LANES), jnp.int32),
        ),
        in_specs=[smem, smem, hbm, hbm, hbm],
        out_specs=(vmem, vmem),
        scratch_shapes=[pltpu.VMEM((rows_dev, width), jnp.float32)] * 3
        + [pltpu.SemaphoreType.DMA((3,))],
        compiler_params=pltpu.CompilerParams(vmem_limit_bytes=54 * 1024 * 1024),
    )(partner, tensor_of_row, master, moment_one, moment_two)
    weights, update, first, second, ratio = pl.pallas_call(
        functools.partial(kernel, groups, subs),
        out_shape=(whole, whole, whole, whole, jax.ShapeDtypeStruct((LAYERS, LANES), jnp.float32)),
        in_specs=[vmem, vmem, hbm],
        out_specs=(vmem, vmem, vmem, vmem, vmem),
        scratch_shapes=[
            pltpu.VMEM((rows_dev, width), jnp.float32),
            pltpu.VMEM(slots, jnp.float32),
            pltpu.VMEM((LAYERS, TILE, LANES), jnp.float32),
            pltpu.VMEM((LAYERS, TILE, LANES), jnp.float32),
            pltpu.VMEM((devices, 1, LANES), jnp.float32),
            pltpu.SemaphoreType.DMA,
            pltpu.SemaphoreType.DMA((devices,)),
            pltpu.SemaphoreType.DMA((devices,)),
            pltpu.SemaphoreType.DMA((devices,)),
            pltpu.SemaphoreType.DMA((devices,)),
        ],
        compiler_params=pltpu.CompilerParams(
            collective_id=0, has_side_effects=True, vmem_limit_bytes=32 * 1024 * 1024
        ),
    )(staged, row_ids, gradient)
    return pl.pallas_call(
        finish,
        out_shape=(whole, whole, whole),
        in_specs=[vmem] * 6,
        out_specs=(hbm, hbm, hbm),
        scratch_shapes=[
            pltpu.VMEM((rows_dev, width), jnp.float32),
            pltpu.SemaphoreType.DMA((PIECES,)),
            pltpu.SemaphoreType.DMA((2,)),
        ],
        compiler_params=pltpu.CompilerParams(vmem_limit_bytes=32 * 1024 * 1024),
    )(ratio, row_ids, weights, update, first, second)


def solution(mesh):
    rows = P(("grp", "sub"), None)
    return jax.shard_map(
        functools.partial(local, mesh.shape["grp"], mesh.shape["sub"]),
        mesh=mesh,
        in_specs=(rows, rows, rows, rows, P(), P()),
        out_specs=(rows, rows, rows),
        check_vma=False,
    )
```

profile of v0, /device:TPU:0, one launch (start us, length us, event | category | flops | bytes accessed | tf_op | source)
XLA Modules:
  0.0 141.0 jit_solution(8903337704589550161)
XLA Ops:
  0.6 0.0 copy-start
  0.6 3.9 %shard_map.85 = (f32[32,3,4,3584]{3,2,1,0:T(4,128)S(1)}, s32[128,128]{1,0:T(8,128)S(1)}) custom-call(s32[32]{0:T(128)} %partner.1, s32[4096]{0:T(1024)} %ids.1, f32[128,3584]{1,0:T(8,128)} %master_hbm.1, f32[128,3584]{1,0:T(8,128)} %one_hbm.1, f32[128,3584]{1,0:T(8,128)} %two_hbm.1), custom_call_target="tpu_custom_call" | custom-call | tf_op jit(solution)/shard_map/pallas_call | solution.py:270
  4.6 0.0 copy-done
  4.6 133.9 %shard_map.86 = (f32[128,3584]{1,0:T(8,128)S(1)}, f32[128,3584]{1,0:T(8,128)S(1)}, f32[128,3584]{1,0:T(8,128)S(1)}, f32[128,3584]{1,0:T(8,128)S(1)}, f32[8,128]{1,0:T(8,128)S(1)}) custom-call(f32[32,3,4,3584]{3,2,1,0:T(4,128)S(1)} %get-tuple-element.10.staged, s32[128,128]{1,0:T(8,128)S(1)} %get-tuple-element.11.row_ids, f32[128,3584]{1,0:T(8,128)S(1)} %copy-done), custom_call_target="tpu_custom_call" | custom-call | tf_op jit(solution)/shard_map/pallas_call | solution.py:282
  138.5 2.5 %shard_map.87 = (f32[128,3584]{1,0:T(8,128)}, f32[128,3584]{1,0:T(8,128)}, f32[128,3584]{1,0:T(8,128)}) custom-call(f32[8,128]{1,0:T(8,128)S(1)} %get-tuple-element.12.ratio_ref, s32[128,128]{1,0:T(8,128)S(1)} %get-tuple-element.11.row_ids, f32[128,3584]{1,0:T(8,128)S(1)} %get-tuple-element.13.weights, f32[128,3584]{1,0:T(8,128)S(1)} %get-tuple-element.14.update, ...), custom_call_target="tpu_custom_call" | custom-call | tf_op jit(solution)/shard_map/pallas_call | solution.py:303
Async XLA Ops:
  0.6 3.9 %copy-start = (f32[128,3584]{1,0:T(8,128)S(1)}, f32[128,3584]{1,0:T(8,128)}, u32[]{:S(2)}) copy-start(f32[128,3584]{1,0:T(8,128)} %grad_hbm.1) | copy-start | bytes 5505028
where the time goes:
time: 141 us
  Pallas kernels  140 us (99%)
    pallas_call x1, Pallas kernels, local(): pl.pallas_call(functools.partial(kernel, groups, subs), out_shape=(whole,...  134 us
    pallas_call x1, Pallas kernels, local(): pl.pallas_call(functools.partial(prepare, groups, subs), out_shape=(pltpu...  3.9 us

commit v1 on v0

v1 whole, which is shorter than its diff:
```python
import functools

import jax
import jax.numpy as jnp
from jax import lax
from jax.experimental import pallas as pl
from jax.experimental.pallas import tpu as pltpu
from jax.sharding import PartitionSpec as P

LAYERS = 8
LANES = 128
TILE = 8
PIECES = 4
MESH = pl.DeviceIdType.MESH

beta_one = 0.9
beta_two = 0.999
step_count = 10
adam_eps = 1e-06
trust_eps = 1e-06
learn_rate = 0.05
decay_rate = 0.01


def xor(a, b, bound):
    total, bit = 0, 1
    while bit < bound:
        total = total + ((a // bit + b // bit) % 2) * bit
        bit *= 2
    return total


def flips(here, bound):
    steps, bit = [], 1
    while bit < bound:
        steps.append(bit - 2 * bit * ((here // bit) % 2))
        bit *= 2
    return [
        here + sum(step for b, step in enumerate(steps) if (k >> b) % 2) for k in range(bound)
    ]


def sub_order(subs):
    width = subs.bit_length() - 1
    codes = [i ^ (i >> 1) for i in range(subs)]
    return [sum(((c >> b) & 1) << (width - 1 - b) for b in range(width)) for c in codes]


def kernel(groups, subs, partner_hbm, ids_hbm, master_hbm, one_hbm, two_hbm, grad_hbm,
           weights, update, first_out, second_out, row_ids, ratio_out,
           partner, ids, master, one, two, grad, staged, landed, acc_w, acc_u, sums,
           load_sem, send_sem, recv_sem, sum_send, sum_recv):
    devices = groups * subs
    rows_dev, width = grad.shape
    block = rows_dev // devices
    many = TILE // block
    columns = width // LANES
    my_grp, my_sub = lax.axis_index("grp"), lax.axis_index("sub")
    me = my_grp * subs + my_sub
    grps, sbs = flips(my_grp, groups), flips(my_sub, subs)
    order = sub_order(subs)
    send_order = order[1:] + order[:1]
    take_order = [s for s in order if s != subs - 1] + [subs - 1]
    peers = [g * subs + s for s in send_order for g in range(groups) if g or s]

    loads = [
        pltpu.make_async_copy(src, dst, load_sem.at[i])
        for i, (src, dst) in enumerate([
            (partner_hbm, partner), (master_hbm, master), (one_hbm, one), (two_hbm, two),
            (ids_hbm, ids), (grad_hbm, grad),
        ])
    ]
    for load in loads:
        load.start()

    def at(k):
        return {"grp": grps[k // subs], "sub": sbs[k % subs]}

    barrier = pltpu.get_barrier_semaphore()
    for k in reversed(peers):
        pl.semaphore_signal(barrier, inc=1, device_id=at(k), device_id_type=MESH)

    def across(g, s):
        return {"grp": xor(my_grp, g, groups), "sub": xor(my_sub, s, subs)}

    def exchange(g, s):
        there, k = across(g, s), g * subs + s
        return pltpu.make_async_remote_copy(
            src_ref=staged.at[k],
            dst_ref=landed.at[k],
            send_sem=send_sem.at[k],
            recv_sem=recv_sem.at[k],
            device_id=there,
            device_id_type=MESH,
        )

    def exchange_sum(k):
        return pltpu.make_async_remote_copy(
            src_ref=sums.at[0],
            dst_ref=sums.at[k],
            send_sem=sum_send.at[k],
            recv_sem=sum_recv.at[k],
            device_id=at(k),
            device_id_type=MESH,
        )

    def rank_of(device):
        def seek(n, found):
            return jnp.where(partner[n] == device, n, found)

        return lax.fori_loop(0, devices, seek, jnp.int32(0), unroll=8)

    def tile_of(place):
        return pl.ds(pl.multiple_of(place // many * TILE, TILE), TILE)

    loads[0].wait()

    def stage(g, s, target):
        there = across(g, s)
        rank = rank_of(there["grp"] * subs + there["sub"])
        slab, part = rank // many, jnp.full((block, LANES), rank % many, jnp.int32)
        for a, source in enumerate((master, one, two)):
            for c in range(columns):
                cut = slice(c * LANES, (c + 1) * LANES)
                tile = source[slab, :, cut]
                piece = tile[:block]
                for i in range(1, many):
                    piece = jnp.where(part == i, tile[i * block : (i + 1) * block], piece)
                target[a, :, cut] = piece

    for load in loads[1:4]:
        load.wait()
    for s in send_order:
        last = 0 if s else 1
        stage(groups - 1, s, staged.at[(groups - 1) * subs + s])
        if s == send_order[0]:
            pl.semaphore_wait(barrier, devices - 1)

        def send(i, carry, s=s):
            g = groups - 1 - i
            stage(g - 1, s, staged.at[(g - 1) * subs + s])
            exchange(g, s).start()
            return carry

        lax.fori_loop(0, groups - 1 - last, send, 0)
        exchange(last, s).start()
    stage(0, 0, landed.at[0])
    my_rank = rank_of(me)
    loads[4].wait()
    loads[5].wait()
    acc_w[...] = jnp.zeros_like(acc_w)
    acc_u[...] = jnp.zeros_like(acc_u)
    sub_iota = lax.broadcasted_iota(jnp.int32, (TILE, LANES), 0)
    lane_iota = lax.broadcasted_iota(jnp.int32, (TILE, LANES), 1)
    scale_one = 1.0 / (1.0 - beta_one**step_count)
    scale_two = 1.0 / (1.0 - beta_two**step_count)

    def consume(g, s):
        there, k = across(g, s), g * subs + s
        source = there["grp"] * subs + there["sub"]
        rows, part = tile_of(source), source % many
        held = sub_iota // block == part
        here = jnp.full((TILE, LANES), -1, jnp.int32)
        for b in range(block):
            tensor = ids[source * rows_dev + my_rank * block + b]
            here = jnp.where(sub_iota == part * block + b, tensor, here)
        row_ids[rows, :] = jnp.where(held, here, row_ids[rows, :])
        sum_w = jnp.zeros((TILE, LANES), jnp.float32)
        sum_u = jnp.zeros((TILE, LANES), jnp.float32)
        for c in range(columns):
            cut = slice(c * LANES, (c + 1) * LANES)

            def arrived(a):
                return jnp.concatenate([landed[k, a, :, cut]] * many, axis=0)

            def put(ref, value):
                ref[rows, cut] = jnp.where(held, value, ref[rows, cut])

            grown = grad[rows, cut]
            w = arrived(0)
            first = beta_one * arrived(1) + (1.0 - beta_one) * grown
            second = beta_two * arrived(2) + (1.0 - beta_two) * grown * grown
            u = (first * scale_one) / (jnp.sqrt(second * scale_two) + adam_eps) + decay_rate * w
            put(first_out, first)
            put(second_out, second)
            put(weights, w)
            put(update, u)
            sum_w += w * w
            sum_u += u * u
        for t in range(LAYERS):
            acc_w[t] += jnp.where(here == t, sum_w, 0.0)
            acc_u[t] += jnp.where(here == t, sum_u, 0.0)

    consume(0, 0)
    for s in take_order:

        def receive(i, carry, s=s):
            g = groups - 1 - i
            exchange(g, s).wait_recv()
            consume(g, s)
            return carry

        lax.fori_loop(0, groups if s else groups - 1, receive, 0)

    col_w = jnp.sum(jnp.sum(acc_w[...], axis=1), axis=1, keepdims=True)
    col_u = jnp.sum(jnp.sum(acc_u[...], axis=1), axis=1, keepdims=True)
    spread = jnp.where(lane_iota == sub_iota, col_w, 0.0) + jnp.where(
        lane_iota == sub_iota + LAYERS, col_u, 0.0
    )
    sums[0] = jnp.sum(spread, axis=0, keepdims=True)
    for k in reversed(peers):
        exchange_sum(k).start()
    for k in peers:
        exchange(k // subs, k % subs).wait_send()
    for k in range(1, devices):
        exchange_sum(k).wait_recv()
    for k in range(1, devices):
        exchange_sum(k).wait_send()
    mine = flips(me, devices)
    total = jnp.zeros((1, LANES), jnp.float32)
    for o in range(devices):
        total = total + sums[mine[o]]
    wide = jnp.broadcast_to(total, (TILE, LANES))
    weight_sq = jnp.sum(jnp.where(lane_iota == sub_iota, wide, 0.0), axis=1, keepdims=True)
    update_sq = jnp.sum(jnp.where(lane_iota == sub_iota + LAYERS, wide, 0.0), axis=1, keepdims=True)
    ratio = learn_rate * (jnp.sqrt(weight_sq) / (jnp.sqrt(update_sq) + trust_eps))
    ratio_out[...] = jnp.broadcast_to(ratio, (TILE, LANES))


def finish(ratio_ref, row_ids, weights, update, first, second,
           fresh_hbm, first_hbm, second_hbm, fresh, fresh_sem, moment_sem):
    rows_dev, width = weights.shape
    columns = width // LANES
    moments = [
        pltpu.make_async_copy(first, first_hbm, moment_sem.at[0]),
        pltpu.make_async_copy(second, second_hbm, moment_sem.at[1]),
    ]
    for move in moments:
        move.start()
    ratio = ratio_ref[...]
    span = rows_dev // PIECES
    moves = []
    for p in range(PIECES):

        def step_rows(s, carry):
            base = pl.multiple_of(p * span + s * TILE, TILE)
            here = row_ids[pl.ds(base, TILE), :]
            step = jnp.zeros((TILE, LANES), jnp.float32)
            for t in range(LAYERS):
                step = jnp.where(here == t, jnp.broadcast_to(ratio[t : t + 1], (TILE, LANES)), step)
            for c in range(columns):
                cut = slice(c * LANES, (c + 1) * LANES)
                rows = pl.ds(base, TILE)
                fresh[rows, cut] = weights[rows, cut] - step * update[rows, cut]
            return carry

        lax.fori_loop(0, span // TILE, step_rows, 0)
        rows = pl.ds(p * span, span)
        moves.append(pltpu.make_async_copy(fresh.at[rows], fresh_hbm.at[rows], fresh_sem.at[p]))
        if p:
            moves[p - 1].start()
    moves[-1].start()
    for move in moves + moments:
        move.wait()


def local(groups, subs, master, moment_one, moment_two, gradient, partner, tensor_of_row):
    rows_dev, width = master.shape
    devices = groups * subs
    block = rows_dev // devices
    whole = jax.ShapeDtypeStruct((rows_dev, width), jnp.float32)
    vmem = pl.BlockSpec(memory_space=pltpu.VMEM)
    hbm = pl.BlockSpec(memory_space=pltpu.HBM)
    slots = (devices, 3, block, width)
    weights, update, first, second, row_ids, ratio = pl.pallas_call(
        functools.partial(kernel, groups, subs),
        out_shape=(
            whole,
            whole,
            whole,
            whole,
            jax.ShapeDtypeStruct((rows_dev, LANES), jnp.int32),
            jax.ShapeDtypeStruct((LAYERS, LANES), jnp.float32),
        ),
        in_specs=[hbm] * 6,
        out_specs=(vmem,) * 6,
        scratch_shapes=[
            pltpu.SMEM(partner.shape, jnp.int32),
            pltpu.SMEM(tensor_of_row.shape, jnp.int32),
        ]
        + [pltpu.VMEM((rows_dev // TILE, TILE, width), jnp.float32)] * 3
        + [
            pltpu.VMEM((rows_dev, width), jnp.float32),
            pltpu.VMEM(slots, jnp.float32),
            pltpu.VMEM(slots, jnp.float32),
            pltpu.VMEM((LAYERS, TILE, LANES), jnp.float32),
            pltpu.VMEM((LAYERS, TILE, LANES), jnp.float32),
            pltpu.VMEM((devices, 1, LANES), jnp.float32),
            pltpu.SemaphoreType.DMA((6,)),
        ]
        + [pltpu.SemaphoreType.DMA((devices,))] * 4,
        compiler_params=pltpu.CompilerParams(
            collective_id=0, has_side_effects=True, vmem_limit_bytes=48 * 1024 * 1024
        ),
    )(
        partner,
        tensor_of_row,
        *(x.reshape(rows_dev // TILE, TILE, width) for x in (master, moment_one, moment_two)),
        gradient,
    )
    return pl.pallas_call(
        finish,
        out_shape=(whole, whole, whole),
        in_specs=[vmem] * 6,
        out_specs=(hbm, hbm, hbm),
        scratch_shapes=[
            pltpu.VMEM((rows_dev, width), jnp.float32),
            pltpu.SemaphoreType.DMA((PIECES,)),
            pltpu.SemaphoreType.DMA((2,)),
        ],
        compiler_params=pltpu.CompilerParams(vmem_limit_bytes=32 * 1024 * 1024),
    )(ratio, row_ids, weights, update, first, second)


def solution(mesh):
    rows = P(("grp", "sub"), None)
    return jax.shard_map(
        functools.partial(local, mesh.shape["grp"], mesh.shape["sub"]),
        mesh=mesh,
        in_specs=(rows, rows, rows, rows, P(), P()),
        out_specs=(rows, rows, rows),
        check_vma=False,
    )
```

time: 141 us -> 140 us (level)
  Pallas kernels: 140 us -> 137 us
  local copies, waits for them, and re-layouts: 0.01 us -> 2.86 us
    pallas_call x1 -> x0, Pallas kernels: 3.9 us -> none  [local(): pl.pallas_call(functools.partial(prepare, groups, subs), out_shape=(pltpu...]
    unnamed x2 -> x6, local copies, waits for them, and re-layouts: 0.01 us -> 2.86 us
where the time goes in v1:
time: 140 us
  Pallas kernels  137 us (98%)
  local copies, waits for them, and re-layouts  2.86 us (2%)
    pallas_call x1, Pallas kernels, local(): pl.pallas_call(functools.partial(kernel, groups, subs), out_shape=(whole,...  134 us
    unnamed x6, local copies, waits for them, and re-layouts  2.86 us

profile of v1, /device:TPU:0, one launch (start us, length us, event | category | flops | bytes accessed | tf_op | source)
XLA Modules:
  0.0 140.2 jit_solution(14932179070990015409)
XLA Ops:
  0.6 0.0 copy-start.1
  0.6 0.7 copy-done.1
  1.4 0.0 copy-start.2
  1.4 0.7 copy-done.2
  2.0 134.2 %shard_map.85 = (f32[128,3584]{1,0:T(8,128)S(1)}, f32[128,3584]{1,0:T(8,128)S(1)}, f32[128,3584]{1,0:T(8,128)S(1)}, f32[128,3584]{1,0:T(8,128)}, s32[128,128]{1,0:T(8,128)S(1)}, /*index=5*/f32[8,128]{1,0:T(8,128)S(1)}) custom-call(s32[32]{0:T(128)S(1)} %copy-done.2, s32[4096]{0:T(1024)S(1)} %copy-done.1, f32[16,8,3584]{2,1,0:T(8,128)} %bitcast.3, ...), custom_call_target="tpu_custom_call" | custom-call | tf_op jit(solution)/shard_map/pallas_call | solution.py:275
  136.2 0.0 copy-start
  136.2 1.5 %copy-done = f32[128,3584]{1,0:T(8,128)S(1)} copy-done((f32[128,3584]{1,0:T(8,128)S(1)}, f32[128,3584]{1,0:T(8,128)}, u32[]{:S(2)}) %copy-start) | copy-done | bytes 1835032
  137.7 2.5 %shard_map.86 = (f32[128,3584]{1,0:T(8,128)}, f32[128,3584]{1,0:T(8,128)}, f32[128,3584]{1,0:T(8,128)}) custom-call(f32[8,128]{1,0:T(8,128)S(1)} %get-tuple-element.9.ratio_ref, s32[128,128]{1,0:T(8,128)S(1)} %get-tuple-element.10.row_ids, f32[128,3584]{1,0:T(8,128)S(1)} %get-tuple-element.11.weights, f32[128,3584]{1,0:T(8,128)S(1)} %get-tuple-element.12.update, ...), custom_call_target="tpu_custom_call" | custom-call | tf_op jit(solution)/shard_map/pallas_call | solution.py:311
Async XLA Ops:
  0.6 0.7 copy-start.1
  1.4 0.7 copy-start.2
  136.2 1.5 %copy-start = (f32[128,3584]{1,0:T(8,128)S(1)}, f32[128,3584]{1,0:T(8,128)}, u32[]{:S(2)}) copy-start(f32[128,3584]{1,0:T(8,128)} %get-tuple-element.14.second) | copy-start | bytes 5505028

commit v2 on v1

--- a/solution.py
+++ b/solution.py
@@ -275,12 +275,9 @@
     weights, update, first, second, row_ids, ratio = pl.pallas_call(
         functools.partial(kernel, groups, subs),
         out_shape=(
-            whole,
-            whole,
-            whole,
-            whole,
-            jax.ShapeDtypeStruct((rows_dev, LANES), jnp.int32),
-            jax.ShapeDtypeStruct((LAYERS, LANES), jnp.float32),
+            *[pltpu.VMEM((rows_dev, width), jnp.float32)] * 4,
+            pltpu.VMEM((rows_dev, LANES), jnp.int32),
+            pltpu.VMEM((LAYERS, LANES), jnp.float32),
         ),
         in_specs=[hbm] * 6,
         out_specs=(vmem,) * 6,
@@ -302,12 +299,15 @@
         compiler_params=pltpu.CompilerParams(
             collective_id=0, has_side_effects=True, vmem_limit_bytes=48 * 1024 * 1024
         ),
-    )(
-        partner,
-        tensor_of_row,
-        *(x.reshape(rows_dev // TILE, TILE, width) for x in (master, moment_one, moment_two)),
-        gradient,
-    )
+    )(*(
+        pltpu.with_memory_space_constraint(x, pltpu.HBM)
+        for x in (
+            partner,
+            tensor_of_row,
+            *(x.reshape(rows_dev // TILE, TILE, width) for x in (master, moment_one, moment_two)),
+            gradient,
+        )
+    ))
     return pl.pallas_call(
         finish,
         out_shape=(whole, whole, whole),

time: 140 us -> 136 us (0.971)
  local copies, waits for them, and re-layouts: 2.86 us -> 0 us
    unnamed x6 -> x0, local copies, waits for them, and re-layouts: 2.86 us -> none
where the time goes in v2:
time: 136 us
  Pallas kernels  136 us (100%)
    pallas_call x1, Pallas kernels, local(): pl.pallas_call(functools.partial(kernel, groups, subs), out_shape=(*[pltp...  133 us

profile of v2, /device:TPU:0, one launch (start us, length us, event | category | flops | bytes accessed | tf_op | source)
XLA Modules:
  0.0 136.3 jit_solution(9671441424295479120)
XLA Ops:
  0.6 133.1 %shard_map.85 = (f32[128,3584]{1,0:T(8,128)S(1)}, f32[128,3584]{1,0:T(8,128)S(1)}, f32[128,3584]{1,0:T(8,128)S(1)}, f32[128,3584]{1,0:T(8,128)S(1)}, s32[128,128]{1,0:T(8,128)S(1)}, /*index=5*/f32[8,128]{1,0:T(8,128)S(1)}) custom-call(s32[32]{0:T(128)} %partner_hbm.1, s32[4096]{0:T(1024)} %ids_hbm.1, f32[16,8,3584]{2,1,0:T(8,128)} %bitcast.3, ...), custom_call_target="tpu_custom_call" | custom-call | tf_op jit(solution)/shard_map/pallas_call | solution.py:275
  133.8 2.5 %shard_map.86 = (f32[128,3584]{1,0:T(8,128)}, f32[128,3584]{1,0:T(8,128)}, f32[128,3584]{1,0:T(8,128)}) custom-call(f32[8,128]{1,0:T(8,128)S(1)} %get-tuple-element.9.ratio_ref, s32[128,128]{1,0:T(8,128)S(1)} %get-tuple-element.10.row_ids, f32[128,3584]{1,0:T(8,128)S(1)} %get-tuple-element.11.weights, f32[128,3584]{1,0:T(8,128)S(1)} %get-tuple-element.12.update, ...), custom_call_target="tpu_custom_call" | custom-call | tf_op jit(solution)/shard_map/pallas_call | solution.py:311

commit v3 on v2

--- a/solution.py
+++ b/solution.py
@@ -11,6 +11,7 @@
 LANES = 128
 TILE = 8
 PIECES = 4
+HELD = 2
 MESH = pl.DeviceIdType.MESH
 
 beta_one = 0.9
@@ -49,7 +50,8 @@
 def kernel(groups, subs, partner_hbm, ids_hbm, master_hbm, one_hbm, two_hbm, grad_hbm,
            weights, update, first_out, second_out, row_ids, ratio_out,
            partner, ids, master, one, two, grad, staged, landed, acc_w, acc_u, sums,
-           load_sem, send_sem, recv_sem, sum_send, sum_recv):
+           near, lent, borrowed, load_sem, send_sem, recv_sem, sum_send, sum_recv,
+           near_sem, lend_send, lend_recv):
     devices = groups * subs
     rows_dev, width = grad.shape
     block = rows_dev // devices
@@ -62,7 +64,24 @@
     send_order = order[1:] + order[:1]
     take_order = [s for s in order if s != subs - 1] + [subs - 1]
     peers = [g * subs + s for s in send_order for g in range(groups) if g or s]
-
+    across_all = subs - 1
+    inner = (my_sub == subs // 2 - 1) | (my_sub == subs // 2)
+    held_back = range(near.shape[0])
+
+    def tile_of(place):
+        return pl.ds(pl.multiple_of(place // many * TILE, TILE), TILE)
+
+    def slot_of(g, s):
+        return grps[g] * subs + sbs[s]
+
+    fetches = [
+        pltpu.make_async_copy(
+            grad_hbm.at[tile_of(slot_of(h, across_all))], near.at[h], near_sem.at[h]
+        )
+        for h in held_back
+    ]
+    for fetch in fetches:
+        fetch.start()
     loads = [
         pltpu.make_async_copy(src, dst, load_sem.at[i])
         for i, (src, dst) in enumerate([
@@ -110,9 +129,29 @@
 
         return lax.fori_loop(0, devices, seek, jnp.int32(0), unroll=8)
 
-    def tile_of(place):
-        return pl.ds(pl.multiple_of(place // many * TILE, TILE), TILE)
-
+    def lend(h):
+        return pltpu.make_async_remote_copy(
+            src_ref=lent.at[h],
+            dst_ref=borrowed.at[h],
+            send_sem=lend_send.at[h],
+            recv_sem=lend_recv.at[h],
+            device_id=at(h * subs + across_all),
+            device_id_type=MESH,
+        )
+
+    def cuts():
+        return [slice(c * LANES, (c + 1) * LANES) for c in range(columns)]
+
+    def pick(tile, part):
+        piece = tile[:block]
+        for i in range(1, many):
+            piece = jnp.where(part == i, tile[i * block : (i + 1) * block], piece)
+        return piece
+
+    for h in held_back:
+        fetches[h].wait()
+        for cut in cuts():
+            lent[h, :, cut] = pick(near[h, :, cut], slot_of(h, across_all) % many)
     loads[0].wait()
 
     def stage(g, s, target):
@@ -120,30 +159,48 @@
         rank = rank_of(there["grp"] * subs + there["sub"])
         slab, part = rank // many, jnp.full((block, LANES), rank % many, jnp.int32)
         for a, source in enumerate((master, one, two)):
-            for c in range(columns):
-                cut = slice(c * LANES, (c + 1) * LANES)
-                tile = source[slab, :, cut]
-                piece = tile[:block]
-                for i in range(1, many):
-                    piece = jnp.where(part == i, tile[i * block : (i + 1) * block], piece)
-                target[a, :, cut] = piece
+            for cut in cuts():
+                target[a, :, cut] = pick(source[slab, :, cut], part)
+
+    pl.semaphore_wait(barrier, devices - 1)
+
+    @pl.when(inner)
+    def _():
+        for h in held_back:
+            lend(h).start()
 
     for load in loads[1:4]:
         load.wait()
     for s in send_order:
         last = 0 if s else 1
-        stage(groups - 1, s, staged.at[(groups - 1) * subs + s])
-        if s == send_order[0]:
-            pl.semaphore_wait(barrier, devices - 1)
-
-        def send(i, carry, s=s):
-            g = groups - 1 - i
-            stage(g - 1, s, staged.at[(g - 1) * subs + s])
-            exchange(g, s).start()
+        turn = my_grp % 2 * (groups // 2) if s else 0
+
+        def step(i, turn=turn):
+            return xor(groups - 1 - i, turn, groups)
+
+        def send_one(g, s=s):
+            if s == across_all:
+                pl.when(jnp.logical_not(inner & (g < len(held_back))))(exchange(g, s).start)
+            else:
+                exchange(g, s).start()
+
+        first_g = step(0)
+        stage(first_g, s, staged.at[first_g * subs + s])
+
+        def send(i, carry, s=s, step=step, send_one=send_one):
+            g, later = step(i), step(i + 1)
+            stage(later, s, staged.at[later * subs + s])
+            send_one(g)
             return carry
 
         lax.fori_loop(0, groups - 1 - last, send, 0)
-        exchange(last, s).start()
+        send_one(step(groups - 1 - last))
+
+    @pl.when(inner)
+    def _():
+        for h in held_back[1:]:
+            exchange(h, across_all).start()
+
     stage(0, 0, landed.at[0])
     my_rank = rank_of(me)
     loads[4].wait()
@@ -155,20 +212,33 @@
     scale_one = 1.0 / (1.0 - beta_one**step_count)
     scale_two = 1.0 / (1.0 - beta_two**step_count)
 
-    def consume(g, s):
+    def moments(w, one, two, grown):
+        first = beta_one * one + (1.0 - beta_one) * grown
+        second = beta_two * two + (1.0 - beta_two) * grown * grown
+        u = (first * scale_one) / (jnp.sqrt(second * scale_two) + adam_eps) + decay_rate * w
+        return first, second, u
+
+    def name_rows(start, part):
+        here = jnp.full((TILE, LANES), -1, jnp.int32)
+        for b in range(block):
+            here = jnp.where(sub_iota == part * block + b, ids[start + b], here)
+        return here
+
+    def account(here, sum_w, sum_u):
+        for t in range(LAYERS):
+            acc_w[t] += jnp.where(here == t, sum_w, 0.0)
+            acc_u[t] += jnp.where(here == t, sum_u, 0.0)
+
+    def consume(g, s, count=True):
         there, k = across(g, s), g * subs + s
         source = there["grp"] * subs + there["sub"]
         rows, part = tile_of(source), source % many
         held = sub_iota // block == part
-        here = jnp.full((TILE, LANES), -1, jnp.int32)
-        for b in range(block):
-            tensor = ids[source * rows_dev + my_rank * block + b]
-            here = jnp.where(sub_iota == part * block + b, tensor, here)
+        here = name_rows(source * rows_dev + my_rank * block, part)
         row_ids[rows, :] = jnp.where(held, here, row_ids[rows, :])
         sum_w = jnp.zeros((TILE, LANES), jnp.float32)
         sum_u = jnp.zeros((TILE, LANES), jnp.float32)
-        for c in range(columns):
-            cut = slice(c * LANES, (c + 1) * LANES)
+        for cut in cuts():
 
             def arrived(a):
                 return jnp.concatenate([landed[k, a, :, cut]] * many, axis=0)
@@ -176,28 +246,54 @@
             def put(ref, value):
                 ref[rows, cut] = jnp.where(held, value, ref[rows, cut])
 
-            grown = grad[rows, cut]
             w = arrived(0)
-            first = beta_one * arrived(1) + (1.0 - beta_one) * grown
-            second = beta_two * arrived(2) + (1.0 - beta_two) * grown * grown
-            u = (first * scale_one) / (jnp.sqrt(second * scale_two) + adam_eps) + decay_rate * w
+            first, second, u = moments(w, arrived(1), arrived(2), grad[rows, cut])
             put(first_out, first)
             put(second_out, second)
             put(weights, w)
             put(update, u)
             sum_w += w * w
             sum_u += u * u
-        for t in range(LAYERS):
-            acc_w[t] += jnp.where(here == t, sum_w, 0.0)
-            acc_u[t] += jnp.where(here == t, sum_u, 0.0)
+        if count:
+            account(here, sum_w, sum_u)
+
+    def count_held(h):
+        k = h * subs + across_all
+        start = me * rows_dev + rank_of(slot_of(h, across_all)) * block
+        sum_w = jnp.zeros((block, LANES), jnp.float32)
+        sum_u = jnp.zeros((block, LANES), jnp.float32)
+        for cut in cuts():
+            w = staged[k, 0, :, cut]
+            _, _, u = moments(w, staged[k, 1, :, cut], staged[k, 2, :, cut], borrowed[h, :, cut])
+            sum_w += w * w
+            sum_u += u * u
+        account(
+            name_rows(start, 0),
+            jnp.concatenate([sum_w] * many, axis=0),
+            jnp.concatenate([sum_u] * many, axis=0),
+        )
 
     consume(0, 0)
     for s in take_order:
+        if s == across_all:
+
+            @pl.when(inner)
+            def _():
+                for h in held_back:
+                    lend(h).wait_recv()
+                    count_held(h)
 
         def receive(i, carry, s=s):
             g = groups - 1 - i
-            exchange(g, s).wait_recv()
-            consume(g, s)
+
+            def take():
+                exchange(g, s).wait_recv()
+                consume(g, s)
+
+            if s == across_all:
+                pl.when(jnp.logical_not(inner & (g < len(held_back))))(take)
+            else:
+                take()
             return carry
 
         lax.fori_loop(0, groups if s else groups - 1, receive, 0)
@@ -210,12 +306,13 @@
     sums[0] = jnp.sum(spread, axis=0, keepdims=True)
     for k in reversed(peers):
         exchange_sum(k).start()
-    for k in peers:
-        exchange(k // subs, k % subs).wait_send()
+
+    @pl.when(inner)
+    def _():
+        exchange(0, across_all).start()
+
     for k in range(1, devices):
         exchange_sum(k).wait_recv()
-    for k in range(1, devices):
-        exchange_sum(k).wait_send()
     mine = flips(me, devices)
     total = jnp.zeros((1, LANES), jnp.float32)
     for o in range(devices):
@@ -225,6 +322,19 @@
     update_sq = jnp.sum(jnp.where(lane_iota == sub_iota + LAYERS, wide, 0.0), axis=1, keepdims=True)
     ratio = learn_rate * (jnp.sqrt(weight_sq) / (jnp.sqrt(update_sq) + trust_eps))
     ratio_out[...] = jnp.broadcast_to(ratio, (TILE, LANES))
+
+    @pl.when(inner)
+    def _():
+        for h in reversed(held_back):
+            exchange(h, across_all).wait_recv()
+            consume(h, across_all, count=False)
+        for h in held_back:
+            lend(h).wait_send()
+
+    for k in peers:
+        exchange(k // subs, k % subs).wait_send()
+    for k in range(1, devices):
+        exchange_sum(k).wait_send()
 
 
 def finish(ratio_ref, row_ids, weights, update, first, second,
@@ -272,6 +382,7 @@
     vmem = pl.BlockSpec(memory_space=pltpu.VMEM)
     hbm = pl.BlockSpec(memory_space=pltpu.HBM)
     slots = (devices, 3, block, width)
+    held_back = min(HELD, groups)
     weights, update, first, second, row_ids, ratio = pl.pallas_call(
         functools.partial(kernel, groups, subs),
         out_shape=(
@@ -293,9 +404,13 @@
             pltpu.VMEM((LAYERS, TILE, LANES), jnp.float32),
             pltpu.VMEM((LAYERS, TILE, LANES), jnp.float32),
             pltpu.VMEM((devices, 1, LANES), jnp.float32),
+            pltpu.VMEM((held_back, TILE, width), jnp.float32),
+            pltpu.VMEM((held_back, block, width), jnp.float32),
+            pltpu.VMEM((held_back, block, width), jnp.float32),
             pltpu.SemaphoreType.DMA((6,)),
         ]
-        + [pltpu.SemaphoreType.DMA((devices,))] * 4,
+        + [pltpu.SemaphoreType.DMA((devices,))] * 4
+        + [pltpu.SemaphoreType.DMA((held_back,))] * 3,
         compiler_params=pltpu.CompilerParams(
             collective_id=0, has_side_effects=True, vmem_limit_bytes=48 * 1024 * 1024
         ),

time: 136 us -> 132 us (0.971)
  Pallas kernels: 136 us -> 131 us
    pallas_call x1, Pallas kernels: 133 us -> 128 us  [local(): pl.pallas_call(functools.partial(kernel, groups, subs), out_shape=(*[pltp...]
where the time goes in v3:
time: 132 us
  Pallas kernels  131 us (99%)
    pallas_call x1, Pallas kernels, local(): pl.pallas_call(functools.partial(kernel, groups, subs), out_shape=(*[pltp...  128 us

profile of v3, /device:TPU:0, one launch (start us, length us, event | category | flops | bytes accessed | tf_op | source)
XLA Modules:
  0.0 131.6 jit_solution(9725358988933890680)
XLA Ops:
  0.6 128.5 %shard_map.85 = (f32[128,3584]{1,0:T(8,128)S(1)}, f32[128,3584]{1,0:T(8,128)S(1)}, f32[128,3584]{1,0:T(8,128)S(1)}, f32[128,3584]{1,0:T(8,128)S(1)}, s32[128,128]{1,0:T(8,128)S(1)}, /*index=5*/f32[8,128]{1,0:T(8,128)S(1)}) custom-call(s32[32]{0:T(128)} %partner_hbm.1, s32[4096]{0:T(1024)} %ids_hbm.1, f32[16,8,3584]{2,1,0:T(8,128)} %bitcast.3, ...), custom_call_target="tpu_custom_call" | custom-call | tf_op jit(solution)/shard_map/pallas_call | solution.py:386
  129.1 2.5 %shard_map.86 = (f32[128,3584]{1,0:T(8,128)}, f32[128,3584]{1,0:T(8,128)}, f32[128,3584]{1,0:T(8,128)}) custom-call(f32[8,128]{1,0:T(8,128)S(1)} %get-tuple-element.9.ratio_ref, s32[128,128]{1,0:T(8,128)S(1)} %get-tuple-element.10.row_ids, f32[128,3584]{1,0:T(8,128)S(1)} %get-tuple-element.11.weights, f32[128,3584]{1,0:T(8,128)S(1)} %get-tuple-element.12.update, ...), custom_call_target="tpu_custom_call" | custom-call | tf_op jit(solution)/shard_map/pallas_call | solution.py:426

commit v4 on v3

--- a/solution.py
+++ b/solution.py
@@ -50,8 +50,8 @@
 def kernel(groups, subs, partner_hbm, ids_hbm, master_hbm, one_hbm, two_hbm, grad_hbm,
            weights, update, first_out, second_out, row_ids, ratio_out,
            partner, ids, master, one, two, grad, staged, landed, acc_w, acc_u, sums,
-           near, lent, borrowed, load_sem, send_sem, recv_sem, sum_send, sum_recv,
-           near_sem, lend_send, lend_recv):
+           near, lent, borrowed, near_sem, partner_sem, ids_sem, grad_sem, send_sem,
+           sum_send, sum_recv, lend_send, lend_recv, load_sem, recv_sem):
     devices = groups * subs
     rows_dev, width = grad.shape
     block = rows_dev // devices
@@ -63,7 +63,7 @@
     order = sub_order(subs)
     send_order = order[1:] + order[:1]
     take_order = [s for s in order if s != subs - 1] + [subs - 1]
-    peers = [g * subs + s for s in send_order for g in range(groups) if g or s]
+    peers = [(g, s) for s in send_order for g in range(groups) if g or s]
     across_all = subs - 1
     inner = (my_sub == subs // 2 - 1) | (my_sub == subs // 2)
     held_back = range(near.shape[0])
@@ -71,55 +71,57 @@
     def tile_of(place):
         return pl.ds(pl.multiple_of(place // many * TILE, TILE), TILE)
 
-    def slot_of(g, s):
+    def device_of(g, s):
         return grps[g] * subs + sbs[s]
 
-    fetches = [
+    for h in held_back:
         pltpu.make_async_copy(
-            grad_hbm.at[tile_of(slot_of(h, across_all))], near.at[h], near_sem.at[h]
-        )
-        for h in held_back
-    ]
-    for fetch in fetches:
-        fetch.start()
-    loads = [
-        pltpu.make_async_copy(src, dst, load_sem.at[i])
-        for i, (src, dst) in enumerate([
-            (partner_hbm, partner), (master_hbm, master), (one_hbm, one), (two_hbm, two),
-            (ids_hbm, ids), (grad_hbm, grad),
-        ])
-    ]
-    for load in loads:
-        load.start()
-
-    def at(k):
-        return {"grp": grps[k // subs], "sub": sbs[k % subs]}
+            grad_hbm.at[tile_of(device_of(h, across_all))], near.at[h], near_sem
+        ).start()
+    pltpu.make_async_copy(partner_hbm, partner, partner_sem).start()
+
+    def at(g, s):
+        return {"grp": grps[g], "sub": sbs[s]}
 
     barrier = pltpu.get_barrier_semaphore()
-    for k in reversed(peers):
-        pl.semaphore_signal(barrier, inc=1, device_id=at(k), device_id_type=MESH)
+    for g, s in peers:
+        pl.semaphore_signal(barrier, inc=1, device_id=at(g, s), device_id_type=MESH)
 
     def across(g, s):
         return {"grp": xor(my_grp, g, groups), "sub": xor(my_sub, s, subs)}
 
     def exchange(g, s):
-        there, k = across(g, s), g * subs + s
+        k = s * groups + g
         return pltpu.make_async_remote_copy(
             src_ref=staged.at[k],
             dst_ref=landed.at[k],
-            send_sem=send_sem.at[k],
-            recv_sem=recv_sem.at[k],
-            device_id=there,
+            send_sem=send_sem,
+            recv_sem=arrival(g, s),
+            device_id=across(g, s),
             device_id_type=MESH,
         )
 
-    def exchange_sum(k):
+    def arrival(g, s):
+        return recv_sem.at[subs + g] if s == across_all else recv_sem.at[s]
+
+    def batch(s, count):
+        run = pl.ds(s * groups + groups - count, count)
+        return pltpu.make_async_remote_copy(
+            src_ref=staged.at[run],
+            dst_ref=landed.at[run],
+            send_sem=send_sem,
+            recv_sem=recv_sem.at[s % subs],
+            device_id=at(1, 0),
+            device_id_type=MESH,
+        )
+
+    def exchange_sum(g, s):
         return pltpu.make_async_remote_copy(
             src_ref=sums.at[0],
-            dst_ref=sums.at[k],
-            send_sem=sum_send.at[k],
-            recv_sem=sum_recv.at[k],
-            device_id=at(k),
+            dst_ref=sums.at[s * groups + g],
+            send_sem=sum_send,
+            recv_sem=sum_recv,
+            device_id=at(g, s),
             device_id_type=MESH,
         )
 
@@ -133,9 +135,9 @@
         return pltpu.make_async_remote_copy(
             src_ref=lent.at[h],
             dst_ref=borrowed.at[h],
-            send_sem=lend_send.at[h],
-            recv_sem=lend_recv.at[h],
-            device_id=at(h * subs + across_all),
+            send_sem=lend_send,
+            recv_sem=lend_recv,
+            device_id=at(h, across_all),
             device_id_type=MESH,
         )
 
@@ -148,11 +150,20 @@
             piece = jnp.where(part == i, tile[i * block : (i + 1) * block], piece)
         return piece
 
+    pltpu.make_async_copy(near, near, near_sem).wait()
+    loads = [
+        pltpu.make_async_copy(src, dst, sem)
+        for src, dst, sem in [
+            (master_hbm, master, load_sem.at[0]), (one_hbm, one, load_sem.at[1]),
+            (two_hbm, two, load_sem.at[2]), (ids_hbm, ids, ids_sem), (grad_hbm, grad, grad_sem),
+        ]
+    ]
+    for load in loads:
+        load.start()
     for h in held_back:
-        fetches[h].wait()
         for cut in cuts():
-            lent[h, :, cut] = pick(near[h, :, cut], slot_of(h, across_all) % many)
-    loads[0].wait()
+            lent[h, :, cut] = pick(near[h, :, cut], device_of(h, across_all) % many)
+    pltpu.make_async_copy(partner_hbm, partner, partner_sem).wait()
 
     def stage(g, s, target):
         there = across(g, s)
@@ -169,7 +180,7 @@
         for h in held_back:
             lend(h).start()
 
-    for load in loads[1:4]:
+    for load in loads[:3]:
         load.wait()
     for s in send_order:
         last = 0 if s else 1
@@ -185,11 +196,11 @@
                 exchange(g, s).start()
 
         first_g = step(0)
-        stage(first_g, s, staged.at[first_g * subs + s])
+        stage(first_g, s, staged.at[s * groups + first_g])
 
         def send(i, carry, s=s, step=step, send_one=send_one):
             g, later = step(i), step(i + 1)
-            stage(later, s, staged.at[later * subs + s])
+            stage(later, s, staged.at[s * groups + later])
             send_one(g)
             return carry
 
@@ -203,8 +214,8 @@
 
     stage(0, 0, landed.at[0])
     my_rank = rank_of(me)
-    loads[4].wait()
-    loads[5].wait()
+    for load in loads[3:]:
+        load.wait()
     acc_w[...] = jnp.zeros_like(acc_w)
     acc_u[...] = jnp.zeros_like(acc_u)
     sub_iota = lax.broadcasted_iota(jnp.int32, (TILE, LANES), 0)
@@ -230,7 +241,7 @@
             acc_u[t] += jnp.where(here == t, sum_u, 0.0)
 
     def consume(g, s, count=True):
-        there, k = across(g, s), g * subs + s
+        there, k = across(g, s), s * groups + g
         source = there["grp"] * subs + there["sub"]
         rows, part = tile_of(source), source % many
         held = sub_iota // block == part
@@ -258,8 +269,8 @@
             account(here, sum_w, sum_u)
 
     def count_held(h):
-        k = h * subs + across_all
-        start = me * rows_dev + rank_of(slot_of(h, across_all)) * block
+        k = across_all * groups + h
+        start = me * rows_dev + rank_of(device_of(h, across_all)) * block
         sum_w = jnp.zeros((block, LANES), jnp.float32)
         sum_u = jnp.zeros((block, LANES), jnp.float32)
         for cut in cuts():
@@ -279,9 +290,19 @@
 
             @pl.when(inner)
             def _():
+                pltpu.make_async_remote_copy(
+                    src_ref=lent,
+                    dst_ref=borrowed,
+                    send_sem=lend_send,
+                    recv_sem=lend_recv,
+                    device_id=at(0, across_all),
+                    device_id_type=MESH,
+                ).wait()
                 for h in held_back:
-                    lend(h).wait_recv()
                     count_held(h)
+
+        else:
+            batch(s, groups if s else groups - 1).wait_recv()
 
         def receive(i, carry, s=s):
             g = groups - 1 - i
@@ -293,7 +314,7 @@
             if s == across_all:
                 pl.when(jnp.logical_not(inner & (g < len(held_back))))(take)
             else:
-                take()
+                consume(g, s)
             return carry
 
         lax.fori_loop(0, groups if s else groups - 1, receive, 0)
@@ -304,19 +325,26 @@
         lane_iota == sub_iota + LAYERS, col_u, 0.0
     )
     sums[0] = jnp.sum(spread, axis=0, keepdims=True)
-    for k in reversed(peers):
-        exchange_sum(k).start()
+    for g, s in peers:
+        exchange_sum(g, s).start()
 
     @pl.when(inner)
     def _():
         exchange(0, across_all).start()
 
-    for k in range(1, devices):
-        exchange_sum(k).wait_recv()
-    mine = flips(me, devices)
+    told = pltpu.make_async_remote_copy(
+        src_ref=sums.at[pl.ds(1, devices - 1)],
+        dst_ref=sums.at[pl.ds(1, devices - 1)],
+        send_sem=sum_send,
+        recv_sem=sum_recv,
+        device_id=at(1, 0),
+        device_id_type=MESH,
+    )
+    told.wait_recv()
     total = jnp.zeros((1, LANES), jnp.float32)
-    for o in range(devices):
-        total = total + sums[mine[o]]
+    for g in range(groups):
+        for s in range(subs):
+            total = total + sums[sbs[s] * groups + grps[g]]
     wide = jnp.broadcast_to(total, (TILE, LANES))
     weight_sq = jnp.sum(jnp.where(lane_iota == sub_iota, wide, 0.0), axis=1, keepdims=True)
     update_sq = jnp.sum(jnp.where(lane_iota == sub_iota + LAYERS, wide, 0.0), axis=1, keepdims=True)
@@ -328,13 +356,16 @@
         for h in reversed(held_back):
             exchange(h, across_all).wait_recv()
             consume(h, across_all, count=False)
-        for h in held_back:
-            lend(h).wait_send()
-
-    for k in peers:
-        exchange(k // subs, k % subs).wait_send()
-    for k in range(1, devices):
-        exchange_sum(k).wait_send()
+
+    pltpu.make_async_remote_copy(
+        src_ref=staged.at[pl.ds(1, devices - 1)],
+        dst_ref=landed.at[pl.ds(1, devices - 1)],
+        send_sem=send_sem,
+        recv_sem=sum_recv,
+        device_id=at(1, 0),
+        device_id_type=MESH,
+    ).wait_send()
+    told.wait_send()
 
 
 def finish(ratio_ref, row_ids, weights, update, first, second,
@@ -407,10 +438,9 @@
             pltpu.VMEM((held_back, TILE, width), jnp.float32),
             pltpu.VMEM((held_back, block, width), jnp.float32),
             pltpu.VMEM((held_back, block, width), jnp.float32),
-            pltpu.SemaphoreType.DMA((6,)),
         ]
-        + [pltpu.SemaphoreType.DMA((devices,))] * 4
-        + [pltpu.SemaphoreType.DMA((held_back,))] * 3,
+        + [pltpu.SemaphoreType.DMA] * 9
+        + [pltpu.SemaphoreType.DMA((3,)), pltpu.SemaphoreType.DMA((subs + groups,))],
         compiler_params=pltpu.CompilerParams(
             collective_id=0, has_side_effects=True, vmem_limit_bytes=48 * 1024 * 1024
         ),

time: 132 us -> 131 us (level)
    pallas_call x1, Pallas kernels: 128 us -> 127 us  [local(): pl.pallas_call(functools.partial(kernel, groups, subs), out_shape=(*[pltp...]
where the time goes in v4:
time: 131 us; the launch traced here: 130 us
  Pallas kernels  130 us (99%)
    pallas_call x1, Pallas kernels, local(): pl.pallas_call(functools.partial(kernel, groups, subs), out_shape=(*[pltp...  127 us

profile of v4, /device:TPU:0, one launch (start us, length us, event | category | flops | bytes accessed | tf_op | source)
XLA Modules:
  0.0 130.2 jit_solution(1981631011688085307)
XLA Ops:
  0.6 127.1 %shard_map.85 = (f32[128,3584]{1,0:T(8,128)S(1)}, f32[128,3584]{1,0:T(8,128)S(1)}, f32[128,3584]{1,0:T(8,128)S(1)}, f32[128,3584]{1,0:T(8,128)S(1)}, s32[128,128]{1,0:T(8,128)S(1)}, /*index=5*/f32[8,128]{1,0:T(8,128)S(1)}) custom-call(s32[32]{0:T(128)} %partner_hbm.1, s32[4096]{0:T(1024)} %ids_hbm.1, f32[16,8,3584]{2,1,0:T(8,128)} %bitcast.3, ...), custom_call_target="tpu_custom_call" | custom-call | tf_op jit(solution)/shard_map/pallas_call | solution.py:417
  127.7 2.5 %shard_map.86 = (f32[128,3584]{1,0:T(8,128)}, f32[128,3584]{1,0:T(8,128)}, f32[128,3584]{1,0:T(8,128)}) custom-call(f32[8,128]{1,0:T(8,128)S(1)} %get-tuple-element.9.ratio_ref, s32[128,128]{1,0:T(8,128)S(1)} %get-tuple-element.10.row_ids, f32[128,3584]{1,0:T(8,128)S(1)} %get-tuple-element.11.weights, f32[128,3584]{1,0:T(8,128)S(1)} %get-tuple-element.12.update, ...), custom_call_target="tpu_custom_call" | custom-call | tf_op jit(solution)/shard_map/pallas_call | solution.py:456

commit v5 on v4

--- a/solution.py
+++ b/solution.py
@@ -11,7 +11,8 @@
 LANES = 128
 TILE = 8
 PIECES = 4
-HELD = 2
+HELD = (2, 2)
+AHEAD = (2, 2)
 MESH = pl.DeviceIdType.MESH
 
 beta_one = 0.9
@@ -47,10 +48,21 @@
     return [sum(((c >> b) & 1) << (width - 1 - b) for b in range(width)) for c in codes]
 
 
+def near_links(groups, subs):
+    bits = [1 << b for b in range(subs.bit_length() - 1)]
+    flat = [(1 << b, 0) for b in range(groups.bit_length() - 1)]
+    flat += [(0, bit) for bit in (bits if subs != 4 else bits[:1])]
+    return flat, [(g, subs - 1) for g in range(2) if (g, subs - 1) not in flat]
+
+
+def diameter(groups, subs):
+    return groups.bit_length() - 1 + (3 if subs == 4 else subs.bit_length() - 1)
+
+
 def kernel(groups, subs, partner_hbm, ids_hbm, master_hbm, one_hbm, two_hbm, grad_hbm,
            weights, update, first_out, second_out, row_ids, ratio_out,
            partner, ids, master, one, two, grad, staged, landed, acc_w, acc_u, sums,
-           near, lent, borrowed, near_sem, partner_sem, ids_sem, grad_sem, send_sem,
+           near, lent, borrowed, rounds, near_sem, partner_sem, ids_sem, grad_sem, send_sem,
            sum_send, sum_recv, lend_send, lend_recv, load_sem, recv_sem):
     devices = groups * subs
     rows_dev, width = grad.shape
@@ -67,6 +79,24 @@
     across_all = subs - 1
     inner = (my_sub == subs // 2 - 1) | (my_sub == subs // 2)
     held_back = range(near.shape[0])
+    odd = my_grp % 2
+
+    def by_core(pair, core):
+        return pair[0] + (pair[1] - pair[0]) * core
+
+    def i_hold(g):
+        return inner & (g < by_core(HELD, odd))
+
+    def peer_holds(g):
+        return inner & (g < by_core(HELD, (odd + g) % 2))
+
+    def send_held(before):
+        ahead = by_core(AHEAD, odd)
+        for h in reversed(held_back):
+            for a in range(3):
+                turn = (by_core(HELD, odd) - 1 - h) * 3 + a
+                now = turn < ahead if before else turn >= ahead
+                pl.when(i_hold(h) & now)(exchange_array(h, across_all, a).start)
 
     def tile_of(place):
         return pl.ds(pl.multiple_of(place // many * TILE, TILE), TILE)
@@ -83,9 +113,29 @@
     def at(g, s):
         return {"grp": grps[g], "sub": sbs[s]}
 
+    flat, steep = near_links(groups, subs)
+    early = min(2, rounds.shape[0])
+
+    def greet(sem):
+        for g, s in flat:
+            pl.semaphore_signal(sem, inc=1, device_id=at(g, s), device_id_type=MESH)
+
+        @pl.when(inner)
+        def _():
+            for g, s in steep:
+                pl.semaphore_signal(sem, inc=1, device_id=at(g, s), device_id_type=MESH)
+
+    def hear(sem):
+        @pl.when(inner)
+        def _():
+            pl.semaphore_wait(sem, len(flat) + len(steep))
+
+        @pl.when(jnp.logical_not(inner))
+        def _():
+            pl.semaphore_wait(sem, len(flat))
+
     barrier = pltpu.get_barrier_semaphore()
-    for g, s in peers:
-        pl.semaphore_signal(barrier, inc=1, device_id=at(g, s), device_id_type=MESH)
+    greet(barrier)
 
     def across(g, s):
         return {"grp": xor(my_grp, g, groups), "sub": xor(my_sub, s, subs)}
@@ -101,6 +151,17 @@
             device_id_type=MESH,
         )
 
+    def exchange_array(g, s, a):
+        k = s * groups + g
+        return pltpu.make_async_remote_copy(
+            src_ref=staged.at[k, a],
+            dst_ref=landed.at[k, a],
+            send_sem=send_sem,
+            recv_sem=arrival(g, s),
+            device_id=across(g, s),
+            device_id_type=MESH,
+        )
+
     def arrival(g, s):
         return recv_sem.at[subs + g] if s == across_all else recv_sem.at[s]
 
@@ -135,8 +196,8 @@
         return pltpu.make_async_remote_copy(
             src_ref=lent.at[h],
             dst_ref=borrowed.at[h],
-            send_sem=lend_send,
-            recv_sem=lend_recv,
+            send_sem=lend_send.at[h],
+            recv_sem=lend_recv.at[h],
             device_id=at(h, across_all),
             device_id_type=MESH,
         )
@@ -158,7 +219,7 @@
             (two_hbm, two, load_sem.at[2]), (ids_hbm, ids, ids_sem), (grad_hbm, grad, grad_sem),
         ]
     ]
-    for load in loads:
+    for load in loads[:3]:
         load.start()
     for h in held_back:
         for cut in cuts():
@@ -173,25 +234,40 @@
             for cut in cuts():
                 target[a, :, cut] = pick(source[slab, :, cut], part)
 
-    pl.semaphore_wait(barrier, devices - 1)
-
-    @pl.when(inner)
-    def _():
-        for h in held_back:
-            lend(h).start()
-
+    hear(barrier)
+    for h in held_back:
+        pl.when(peer_holds(h))(lend(h).start)
+
+    for r in range(early):
+        greet(rounds.at[r])
+        hear(rounds.at[r])
+    if early < rounds.shape[0]:
+        greet(rounds.at[early])
     for load in loads[:3]:
         load.wait()
+    for load in loads[3:]:
+        load.start()
+    for g in range(2):
+        stage(g, send_order[0], staged.at[send_order[0] * groups + g])
+    for g in range(2):
+        exchange(g, send_order[0]).start()
+    for r in range(early, rounds.shape[0]):
+        hear(rounds.at[r])
+        if r + 1 < rounds.shape[0]:
+            greet(rounds.at[r + 1])
     for s in send_order:
-        last = 0 if s else 1
-        turn = my_grp % 2 * (groups // 2) if s else 0
-
-        def step(i, turn=turn):
-            return xor(groups - 1 - i, turn, groups)
+        begin = 2 if s == send_order[0] else 0 if s else 1
+        if begin == groups:
+            continue
+
+        def step(i, s=s, begin=begin):
+            if s == send_order[0]:
+                return 2 + (groups - 3 - i + odd * 4) % (groups - 2)
+            return xor(groups - 1 - i, odd * (groups // 2), groups) if s else groups - 1 - i
 
         def send_one(g, s=s):
             if s == across_all:
-                pl.when(jnp.logical_not(inner & (g < len(held_back))))(exchange(g, s).start)
+                pl.when(jnp.logical_not(i_hold(g)))(exchange(g, s).start)
             else:
                 exchange(g, s).start()
 
@@ -204,13 +280,10 @@
             send_one(g)
             return carry
 
-        lax.fori_loop(0, groups - 1 - last, send, 0)
-        send_one(step(groups - 1 - last))
-
-    @pl.when(inner)
-    def _():
-        for h in held_back[1:]:
-            exchange(h, across_all).start()
+        lax.fori_loop(0, groups - 1 - begin, send, 0)
+        send_one(step(groups - 1 - begin))
+
+    send_held(True)
 
     stage(0, 0, landed.at[0])
     my_rank = rank_of(me)
@@ -288,17 +361,11 @@
     for s in take_order:
         if s == across_all:
 
-            @pl.when(inner)
-            def _():
-                pltpu.make_async_remote_copy(
-                    src_ref=lent,
-                    dst_ref=borrowed,
-                    send_sem=lend_send,
-                    recv_sem=lend_recv,
-                    device_id=at(0, across_all),
-                    device_id_type=MESH,
-                ).wait()
-                for h in held_back:
+            for h in held_back:
+
+                @pl.when(i_hold(h))
+                def _(h=h):
+                    lend(h).wait_recv()
                     count_held(h)
 
         else:
@@ -312,7 +379,7 @@
                 consume(g, s)
 
             if s == across_all:
-                pl.when(jnp.logical_not(inner & (g < len(held_back))))(take)
+                pl.when(jnp.logical_not(peer_holds(g)))(take)
             else:
                 consume(g, s)
             return carry
@@ -328,9 +395,7 @@
     for g, s in peers:
         exchange_sum(g, s).start()
 
-    @pl.when(inner)
-    def _():
-        exchange(0, across_all).start()
+    send_held(False)
 
     told = pltpu.make_async_remote_copy(
         src_ref=sums.at[pl.ds(1, devices - 1)],
@@ -351,11 +416,13 @@
     ratio = learn_rate * (jnp.sqrt(weight_sq) / (jnp.sqrt(update_sq) + trust_eps))
     ratio_out[...] = jnp.broadcast_to(ratio, (TILE, LANES))
 
-    @pl.when(inner)
-    def _():
-        for h in reversed(held_back):
+    for h in reversed(held_back):
+
+        @pl.when(peer_holds(h))
+        def _(h=h):
             exchange(h, across_all).wait_recv()
             consume(h, across_all, count=False)
+            lend(h).wait_send()
 
     pltpu.make_async_remote_copy(
         src_ref=staged.at[pl.ds(1, devices - 1)],
@@ -413,7 +480,7 @@
     vmem = pl.BlockSpec(memory_space=pltpu.VMEM)
     hbm = pl.BlockSpec(memory_space=pltpu.HBM)
     slots = (devices, 3, block, width)
-    held_back = min(HELD, groups)
+    held_back = max(HELD)
     weights, update, first, second, row_ids, ratio = pl.pallas_call(
         functools.partial(kernel, groups, subs),
         out_shape=(
@@ -439,7 +506,9 @@
             pltpu.VMEM((held_back, block, width), jnp.float32),
             pltpu.VMEM((held_back, block, width), jnp.float32),
         ]
-        + [pltpu.SemaphoreType.DMA] * 9
+        + [pltpu.SemaphoreType.REGULAR((diameter(groups, subs) - 1,))]
+        + [pltpu.SemaphoreType.DMA] * 7
+        + [pltpu.SemaphoreType.DMA((held_back,))] * 2
         + [pltpu.SemaphoreType.DMA((3,)), pltpu.SemaphoreType.DMA((subs + groups,))],
         compiler_params=pltpu.CompilerParams(
             collective_id=0, has_side_effects=True, vmem_limit_bytes=48 * 1024 * 1024

time: 131 us -> 130 us (level)
  Pallas kernels: 130 us -> 128 us
    pallas_call x1, Pallas kernels: 127 us -> 126 us  [local(): pl.pallas_call(functools.partial(kernel, groups, subs), out_shape=(*[pltp...]
where the time goes in v5:
time: 130 us; the launch traced here: 129 us
  Pallas kernels  128 us (98%)
    pallas_call x1, Pallas kernels, local(): pl.pallas_call(functools.partial(kernel, groups, subs), out_shape=(*[pltp...  126 us

profile of v5, /device:TPU:0, one launch (start us, length us, event | category | flops | bytes accessed | tf_op | source)
XLA Modules:
  0.0 128.8 jit_solution(11216630092994192436)
XLA Ops:
  0.6 125.6 %shard_map.85 = (f32[128,3584]{1,0:T(8,128)S(1)}, f32[128,3584]{1,0:T(8,128)S(1)}, f32[128,3584]{1,0:T(8,128)S(1)}, f32[128,3584]{1,0:T(8,128)S(1)}, s32[128,128]{1,0:T(8,128)S(1)}, /*index=5*/f32[8,128]{1,0:T(8,128)S(1)}) custom-call(s32[32]{0:T(128)} %partner_hbm.1, s32[4096]{0:T(1024)} %ids_hbm.1, f32[16,8,3584]{2,1,0:T(8,128)} %bitcast.3, ...), custom_call_target="tpu_custom_call" | custom-call | tf_op jit(solution)/shard_map/pallas_call | solution.py:484
  126.3 2.5 %shard_map.86 = (f32[128,3584]{1,0:T(8,128)}, f32[128,3584]{1,0:T(8,128)}, f32[128,3584]{1,0:T(8,128)}) custom-call(f32[8,128]{1,0:T(8,128)S(1)} %get-tuple-element.9.ratio_ref, s32[128,128]{1,0:T(8,128)S(1)} %get-tuple-element.10.row_ids, f32[128,3584]{1,0:T(8,128)S(1)} %get-tuple-element.11.weights, f32[128,3584]{1,0:T(8,128)S(1)} %get-tuple-element.12.update, ...), custom_call_target="tpu_custom_call" | custom-call | tf_op jit(solution)/shard_map/pallas_call | solution.py:525

commit v6 on v5

--- a/solution.py
+++ b/solution.py
@@ -114,7 +114,6 @@
         return {"grp": grps[g], "sub": sbs[s]}
 
     flat, steep = near_links(groups, subs)
-    early = min(2, rounds.shape[0])
 
     def greet(sem):
         for g, s in flat:
@@ -238,23 +237,26 @@
     for h in held_back:
         pl.when(peer_holds(h))(lend(h).start)
 
-    for r in range(early):
-        greet(rounds.at[r])
+    last_round = rounds.shape[0] - 1
+
+    def next_round(r):
         hear(rounds.at[r])
-    if early < rounds.shape[0]:
-        greet(rounds.at[early])
+        if r < last_round:
+            greet(rounds.at[r + 1])
+
+    greet(rounds.at[0])
+    next_round(0)
     for load in loads[:3]:
         load.wait()
     for load in loads[3:]:
         load.start()
     for g in range(2):
         stage(g, send_order[0], staged.at[send_order[0] * groups + g])
-    for g in range(2):
-        exchange(g, send_order[0]).start()
-    for r in range(early, rounds.shape[0]):
-        hear(rounds.at[r])
-        if r + 1 < rounds.shape[0]:
-            greet(rounds.at[r + 1])
+    exchange(0, send_order[0]).start()
+    next_round(1)
+    exchange(1, send_order[0]).start()
+    for r in range(2, last_round + 1):
+        next_round(r)
     for s in send_order:
         begin = 2 if s == send_order[0] else 0 if s else 1
         if begin == groups:

time: 130 us -> 129 us (level)
  no operation moved by 1% of the time
where the time goes in v6:
time: 129 us
  Pallas kernels  128 us (99%)
    pallas_call x1, Pallas kernels, local(): pl.pallas_call(functools.partial(kernel, groups, subs), out_shape=(*[pltp...  126 us

profile of v6, /device:TPU:0, one launch (start us, length us, event | category | flops | bytes accessed | tf_op | source)
XLA Modules:
  0.0 128.6 jit_solution(12186902894475745139)
XLA Ops:
  0.6 125.5 %shard_map.85 = (f32[128,3584]{1,0:T(8,128)S(1)}, f32[128,3584]{1,0:T(8,128)S(1)}, f32[128,3584]{1,0:T(8,128)S(1)}, f32[128,3584]{1,0:T(8,128)S(1)}, s32[128,128]{1,0:T(8,128)S(1)}, /*index=5*/f32[8,128]{1,0:T(8,128)S(1)}) custom-call(s32[32]{0:T(128)} %partner_hbm.1, s32[4096]{0:T(1024)} %ids_hbm.1, f32[16,8,3584]{2,1,0:T(8,128)} %bitcast.3, ...), custom_call_target="tpu_custom_call" | custom-call | tf_op jit(solution)/shard_map/pallas_call | solution.py:486
  126.2 2.5 %shard_map.86 = (f32[128,3584]{1,0:T(8,128)}, f32[128,3584]{1,0:T(8,128)}, f32[128,3584]{1,0:T(8,128)}) custom-call(f32[8,128]{1,0:T(8,128)S(1)} %get-tuple-element.9.ratio_ref, s32[128,128]{1,0:T(8,128)S(1)} %get-tuple-element.10.row_ids, f32[128,3584]{1,0:T(8,128)S(1)} %get-tuple-element.11.weights, f32[128,3584]{1,0:T(8,128)S(1)} %get-tuple-element.12.update, ...), custom_call_target="tpu_custom_call" | custom-call | tf_op jit(solution)/shard_map/pallas_call | solution.py:527

commit v7 on v6

--- a/solution.py
+++ b/solution.py
@@ -12,7 +12,7 @@
 TILE = 8
 PIECES = 4
 HELD = (2, 2)
-AHEAD = (2, 2)
+AHEAD = (2, 3)
 MESH = pl.DeviceIdType.MESH
 
 beta_one = 0.9
@@ -265,7 +265,7 @@
         def step(i, s=s, begin=begin):
             if s == send_order[0]:
                 return 2 + (groups - 3 - i + odd * 4) % (groups - 2)
-            return xor(groups - 1 - i, odd * (groups // 2), groups) if s else groups - 1 - i
+            return xor(groups - 1 - i, odd * (groups // 4), groups) if s else groups - 1 - i
 
         def send_one(g, s=s):
             if s == across_all:

time: 129 us -> 129 us (level)
  no operation moved by 1% of the time
where the time goes in v7:
time: 129 us
  Pallas kernels  128 us (99%)
    pallas_call x1, Pallas kernels, local(): pl.pallas_call(functools.partial(kernel, groups, subs), out_shape=(*[pltp...  126 us

profile of v7, /device:TPU:0, one launch (start us, length us, event | category | flops | bytes accessed | tf_op | source)
XLA Modules:
  0.0 128.9 jit_solution(2402359941210029604)
XLA Ops:
  0.6 125.7 %shard_map.85 = (f32[128,3584]{1,0:T(8,128)S(1)}, f32[128,3584]{1,0:T(8,128)S(1)}, f32[128,3584]{1,0:T(8,128)S(1)}, f32[128,3584]{1,0:T(8,128)S(1)}, s32[128,128]{1,0:T(8,128)S(1)}, /*index=5*/f32[8,128]{1,0:T(8,128)S(1)}) custom-call(s32[32]{0:T(128)} %partner_hbm.1, s32[4096]{0:T(1024)} %ids_hbm.1, f32[16,8,3584]{2,1,0:T(8,128)} %bitcast.3, ...), custom_call_target="tpu_custom_call" | custom-call | tf_op jit(solution)/shard_map/pallas_call | solution.py:486
  126.4 2.5 %shard_map.86 = (f32[128,3584]{1,0:T(8,128)}, f32[128,3584]{1,0:T(8,128)}, f32[128,3584]{1,0:T(8,128)}) custom-call(f32[8,128]{1,0:T(8,128)S(1)} %get-tuple-element.9.ratio_ref, s32[128,128]{1,0:T(8,128)S(1)} %get-tuple-element.10.row_ids, f32[128,3584]{1,0:T(8,128)S(1)} %get-tuple-element.11.weights, f32[128,3584]{1,0:T(8,128)S(1)} %get-tuple-element.12.update, ...), custom_call_target="tpu_custom_call" | custom-call | tf_op jit(solution)/shard_map/pallas_call | solution.py:527
